TPU v7x, 32 devices: a whole 2x2x4 slice. The times are simulated.
32 devices in a mesh: ty: 4 (over x, core), tx: 8 (over z, y).
Axes of the slice: x: 2, y: 2, z: 4, core: 2. Of those that a mesh axis runs over, the one named last changes fastest.
Arguments:
- potential_warmth: float32 [16, 512, 4096], P(None, ('ty', 'tx')), may hold values from -2 to 30
- saltiness_field: float32 [16, 512, 4096], P(None, ('ty', 'tx')), may hold values from 30 to 38
- ocean_tier_tally: int32 [512, 4096], P(('ty', 'tx')), may hold values from 0 to 16, as said below
Outputs:
- buoyancy_anomaly: float32 [16, 512, 4096], P(None, 'ty', 'tx')
- laplacian: float32 [16, 512, 4096], P(None, 'ty', 'tx')
Inputs may be any that keep to these rules, and one draw needn't show every extreme that they name: `ocean_tier_tally`: columns with 0 are land; the tile of rows 0 .. 127 and columns 0 .. 511 is land in every draw, and other whole tiles of land occur. Within the rows of one device and the columns of one tile, at most 6144 columns are ocean, and some such block has exactly 6144.
All inputs are finite; a program needn't handle non-finite values.
Results may differ from a plain program's by a relative error of at most 0.00002.
Values sent between devices are 32-bit elements; how exact they have to be, the bound alone decides.
A program may use at most 128 MiB of HBM per device.

v0:
```python
import functools

import jax
import jax.numpy as jnp
from jax import lax
from jax.experimental import pallas as pl
from jax.experimental.pallas import tpu as pltpu
from jax.sharding import PartitionSpec as P

therm_coef = 0.1655
haline_coef = 0.76554
cabbel_coef = 0.05952
haline_second = 0.00054914
thermo_press = 0.0001497
haline_press = 1.109e-05
cross_coef = 0.0024341

MESH = pl.DeviceIdType.MESH
LANES = 128
MIB = 1 << 20


def density(warmth, salt, wet, height):
    heat = warmth - 10.0
    haline = salt - 35.0
    anomaly = -therm_coef * (1.0 + 0.5 * cabbel_coef * heat + thermo_press * height) * heat
    anomaly = anomaly + haline_coef * (1.0 - 0.5 * haline_second * haline - haline_press * height) * haline
    anomaly = anomaly - cross_coef * heat * haline
    return jnp.where(wet, anomaly, 0.0)


def exchange(
    ny, nx, groups,
    warmth_ref, salt_ref, tally_ref,
    tile_ref, bottom_ref, sides_ref, north_ref, south_ref, fold_ref,
    warmth, salt, tally, dens, pack, slab, slab_bottom, low, high,
    load_sem, send_sem, recv_sem, bsend_sem, brecv_sem, psend_sem, precv_sem, own_sem, slab_sem, hsend_sem, hrecv_sem,
):
    y, x = lax.axis_index("ty"), lax.axis_index("tx")
    levels, band, width = dens.shape
    wide = width // nx
    depth = levels // groups
    up, down = lax.rem(y + 1, ny), lax.rem(y + ny - 1, ny)
    last = y == ny - 1

    loads = []
    for g in range(groups):
        part = pl.ds(g * depth, depth)
        pair = [
            pltpu.make_async_copy(warmth_ref.at[part], warmth.at[part], load_sem.at[2 * g]),
            pltpu.make_async_copy(salt_ref.at[part], salt.at[part], load_sem.at[2 * g + 1]),
        ]
        if g == 0:
            load_tally = pltpu.make_async_copy(tally_ref, tally, load_sem.at[2 * groups])
            load_tally.start()
        for copy in pair:
            copy.start()
        loads.append(pair)

    barrier = pltpu.get_barrier_semaphore()
    for m in range(1, nx):
        pl.semaphore_signal(barrier, inc=1, device_id=(y, x ^ m), device_id_type=MESH)
    for other in (up, down):
        pl.semaphore_signal(barrier, inc=1, device_id=(other, x), device_id_type=MESH)

    def columns(t):
        return pl.ds(pl.multiple_of(t * wide, LANES), wide)

    def rows(t):
        return pl.ds(pl.multiple_of(t * band, 8), band)

    mine = rows(x)

    def bottom_copy(m):
        t = x ^ m
        return pltpu.make_async_remote_copy(
            src_ref=tally_ref.at[:, columns(t)], dst_ref=bottom_ref.at[mine],
            send_sem=bsend_sem.at[m], recv_sem=brecv_sem.at[x], device_id=(y, t), device_id_type=MESH)

    def dens_copy(g, m):
        t = x ^ m
        part = pl.ds(g * depth, depth)
        return pltpu.make_async_remote_copy(
            src_ref=dens.at[part, :, columns(t)], dst_ref=tile_ref.at[part, mine],
            send_sem=send_sem.at[g, m], recv_sem=recv_sem.at[g, x], device_id=(y, t), device_id_type=MESH)

    def pack_copy(m):
        t = x ^ m
        return pltpu.make_async_remote_copy(
            src_ref=pack.at[t], dst_ref=sides_ref.at[mine],
            send_sem=psend_sem.at[m], recv_sem=precv_sem.at[x], device_id=(y, t), device_id_type=MESH)

    own = [
        pltpu.make_async_copy(dens.at[:, :, columns(x)], tile_ref.at[:, mine], own_sem.at[0]),
        pltpu.make_async_copy(tally_ref.at[:, columns(x)], bottom_ref.at[mine], own_sem.at[1]),
        pltpu.make_async_copy(pack.at[x], sides_ref.at[mine], own_sem.at[2]),
    ]
    far = [m for m in range(nx - 1, 0, -1) if m >= nx // 2]
    near = [m for m in range(nx - 1, 0, -1) if m < nx // 2]

    pl.semaphore_wait(barrier, nx - 1 + 2)
    for m in far + near:
        bottom_copy(m).start()
    own[1].start()
    load_tally.wait()

    lane = lax.broadcasted_iota(jnp.int32, (band, LANES), 1)

    def fill(t, _):
        before = lax.rem(t + nx - 1, nx)
        after = lax.rem(t + 1, nx)
        left = tally[:, pl.ds(pl.multiple_of(before * wide + wide - LANES, LANES), LANES)].astype(jnp.float32)
        right = tally[:, pl.ds(pl.multiple_of(after * wide, LANES), LANES)].astype(jnp.float32)
        cells = jnp.where(lane == 2 * levels, jnp.broadcast_to(left[:, LANES - 1:], (band, LANES)), 0.0)
        cells = jnp.where(lane == 2 * levels + 1, jnp.broadcast_to(right[:, :1], (band, LANES)), cells)
        pack[t] = cells
        return 0

    lax.fori_loop(0, nx, fill, 0)

    def level(k, _):
        height = 5.0 + 10.0 * k.astype(jnp.float32)

        def block(t, _):
            cols = columns(t)
            value = density(warmth[k, :, cols], salt[k, :, cols], k < tally[:, cols], height)
            dens[k, :, cols] = value
            after = lax.rem(t + 1, nx)
            before = lax.rem(t + nx - 1, nx)
            pack[after] = jnp.where(lane == k, jnp.broadcast_to(value[:, wide - 1:], (band, LANES)), pack[after])
            pack[before] = jnp.where(lane == levels + k, jnp.broadcast_to(value[:, :1], (band, LANES)), pack[before])
            return 0

        lax.fori_loop(0, nx, block, 0)
        return 0

    for g in range(groups):
        for copy in loads[g]:
            copy.wait()
        lax.fori_loop(g * depth, (g + 1) * depth, level, 0)
        for m in far:
            dens_copy(g, m).start()
    own[0].start()
    own[2].start()
    for g in range(groups):
        for m in near:
            dens_copy(g, m).start()
    for m in far + near:
        pack_copy(m).start()

    own[0].wait()
    own[1].wait()

    def arrive(s):
        @pl.when(x != s)
        def _():
            pltpu.make_async_copy(bottom_ref.at[rows(s)], bottom_ref.at[rows(s)], brecv_sem.at[s]).wait()
            for g in range(groups):
                part = tile_ref.at[pl.ds(g * depth, depth), rows(s)]
                pltpu.make_async_copy(part, part, recv_sem.at[g, s]).wait()

    arrive(0)
    arrive(nx - 1)
    top = nx * band - 8
    slabs = [
        pltpu.make_async_copy(tile_ref.at[:, pl.ds(0, 8)], slab.at[0], slab_sem.at[0]),
        pltpu.make_async_copy(tile_ref.at[:, pl.ds(top, 8)], slab.at[1], slab_sem.at[1]),
        pltpu.make_async_copy(bottom_ref.at[pl.ds(0, 8)], slab_bottom.at[0], slab_sem.at[2]),
        pltpu.make_async_copy(bottom_ref.at[pl.ds(top, 8)], slab_bottom.at[1], slab_sem.at[3]),
    ]
    for copy in slabs:
        copy.start()
    for copy in slabs:
        copy.wait()
    for k in range(levels):
        low[k:k + 1, :] = slab[0, k, 0:1, :]
        high[k:k + 1, :] = slab[1, k, 7:8, :]
    low[levels:, :] = jnp.broadcast_to(slab_bottom[0, 0:1, :].astype(jnp.float32), (8, wide))
    high[levels:, :] = jnp.broadcast_to(slab_bottom[1, 7:8, :].astype(jnp.float32), (8, wide))

    def halo(index, src, dst, target):
        return pltpu.make_async_remote_copy(
            src_ref=src, dst_ref=dst, send_sem=hsend_sem.at[index], recv_sem=hrecv_sem.at[index],
            device_id=target, device_id_type=MESH)

    to_south = halo(0, low, north_ref, (down, x))
    to_north = halo(1, high, south_ref, (up, x))
    across = halo(2, high, fold_ref, (y, x ^ (nx - 1)))
    to_south.start()
    to_north.start()

    @pl.when(last)
    def _():
        across.start()

    for s in range(1, nx - 1):
        arrive(s)
    for s in range(nx):
        @pl.when(x != s)
        def _():
            pltpu.make_async_copy(sides_ref.at[rows(s)], sides_ref.at[rows(s)], precv_sem.at[s]).wait()
    own[2].wait()
    to_south.wait()
    to_north.wait()

    @pl.when(last)
    def _():
        across.wait()

    for m in far + near:
        bottom_copy(m).wait_send()
        pack_copy(m).wait_send()
        for g in range(groups):
            dens_copy(g, m).wait_send()


def stencil(
    ny, levels, per,
    tile_ref, bottom_ref, sides_ref, north_ref, south_ref, fold_ref,
    dens_ref, lap_ref,
    north, south, bottoms,
):
    y = lax.axis_index("ty")
    tall, wide = bottom_ref.shape
    row = lax.broadcasted_iota(jnp.int32, (tall, wide), 0)
    col = lax.broadcasted_iota(jnp.int32, (tall, wide), 1)
    side_lane = lax.broadcasted_iota(jnp.int32, sides_ref.shape, 1)

    def side(index):
        return jnp.sum(jnp.where(side_lane == index, sides_ref[...], 0.0), axis=1, keepdims=True)

    def around(cells, top, base, left, right):
        above = jnp.where(row == tall - 1, top, pltpu.roll(cells, tall - 1, 0))
        below = jnp.where(row == 0, base, pltpu.roll(cells, 1, 0))
        east = jnp.where(col == wide - 1, right, pltpu.roll(cells, wide - 1, 1))
        west = jnp.where(col == 0, left, pltpu.roll(cells, 1, 1))
        return above, below, east, west

    @pl.when(pl.program_id(0) == 0)
    def _():
        mirror = fold_ref[...]
        lane = lax.broadcasted_iota(jnp.int32, mirror.shape, 1)
        bit = 1
        while bit < wide:
            mirror = jnp.where((lane & bit) != 0, pltpu.roll(mirror, bit, 1), pltpu.roll(mirror, wide - bit, 1))
            bit *= 2
        north[...] = jnp.where(y == ny - 1, mirror, north_ref[...])
        south[...] = jnp.where(y == 0, 0.0, south_ref[...])
        own = bottom_ref[...].astype(jnp.float32)
        near = around(own, north[levels:levels + 1, :], south[levels:levels + 1, :], side(2 * levels), side(2 * levels + 1))
        bottoms[0] = own
        for index in range(4):
            bottoms[index + 1] = near[index]

    for j in range(per):
        k = pl.program_id(0) * per + j
        number = k.astype(jnp.float32)
        cells = tile_ref[j]
        near = around(cells, north[pl.ds(k, 1), :], south[pl.ds(k, 1), :], side(k), side(levels + k))
        count = jnp.where(number < bottoms[1], 1.0, 0.0)
        for index in range(2, 5):
            count = count + jnp.where(number < bottoms[index], 1.0, 0.0)
        total = (near[0] + near[1]) + (near[2] + near[3]) - count * cells
        dens_ref[j] = cells
        lap_ref[j] = jnp.where(number < bottoms[0], total, 0.0)


def on_device(ny, nx, potential_warmth, saltiness_field, ocean_tier_tally):
    levels, band, width = potential_warmth.shape
    wide, tall = width // nx, band * nx
    groups = 4 if levels % 4 == 0 else 1
    hbm = pl.BlockSpec(memory_space=pl.ANY)
    f32, i32 = jnp.float32, jnp.int32
    edge = jax.ShapeDtypeStruct((levels + 8, wide), f32)
    dma = pltpu.SemaphoreType.DMA
    parts = pl.pallas_call(
        functools.partial(exchange, ny, nx, groups),
        out_shape=(
            jax.ShapeDtypeStruct((levels, tall, wide), f32),
            jax.ShapeDtypeStruct((tall, wide), i32),
            jax.ShapeDtypeStruct((tall, LANES), f32),
            edge, edge, edge,
        ),
        in_specs=[hbm] * 3,
        out_specs=(hbm,) * 6,
        scratch_shapes=[
            pltpu.VMEM((levels, band, width), f32),
            pltpu.VMEM((levels, band, width), f32),
            pltpu.VMEM((band, width), i32),
            pltpu.VMEM((levels, band, width), f32),
            pltpu.VMEM((nx, band, LANES), f32),
            pltpu.VMEM((2, levels, 8, wide), f32),
            pltpu.VMEM((2, 8, wide), i32),
            pltpu.VMEM((levels + 8, wide), f32),
            pltpu.VMEM((levels + 8, wide), f32),
            dma((2 * groups + 1,)),
            dma((groups, nx)), dma((groups, nx)),
            dma((nx,)), dma((nx,)), dma((nx,)), dma((nx,)),
            dma((3,)), dma((4,)), dma((3,)), dma((3,)),
        ],
        compiler_params=pltpu.CompilerParams(collective_id=0, has_side_effects=True, vmem_limit_bytes=24 * MIB),
        cost_estimate=pl.CostEstimate(flops=0, bytes_accessed=16 * levels * band * width, transcendentals=0),
        name="exchange",
    )(potential_warmth, saltiness_field, ocean_tier_tally)
    per = 2 if levels % 2 == 0 else 1
    block = pl.BlockSpec((per, tall, wide), lambda i: (i, 0, 0))
    whole = pl.BlockSpec(memory_space=pltpu.VMEM)
    out = jax.ShapeDtypeStruct((levels, tall, wide), f32)
    return pl.pallas_call(
        functools.partial(stencil, ny, levels, per),
        grid=(levels // per,),
        out_shape=(out, out),
        in_specs=[block] + [whole] * 5,
        out_specs=(block, block),
        scratch_shapes=[
            pltpu.VMEM((levels + 8, wide), f32),
            pltpu.VMEM((levels + 8, wide), f32),
            pltpu.VMEM((5, tall, wide), f32),
        ],
        compiler_params=pltpu.CompilerParams(vmem_limit_bytes=24 * MIB),
        name="stencil",
    )(*parts)


def solution(mesh):
    placed = (P(None, ("ty", "tx"), None), P(None, ("ty", "tx"), None), P(("ty", "tx"), None))
    return jax.shard_map(
        functools.partial(on_device, mesh.shape["ty"], mesh.shape["tx"]),
        mesh=mesh,
        in_specs=placed,
        out_specs=(P(None, "ty", "tx"), P(None, "ty", "tx")),
        check_vma=False,
    )
```

profile of v0, /device:TPU:1, one launch (start us, length us, event | category | flops | bytes accessed | tf_op | source)
XLA Modules:
  0.0 119.5 jit_solution(13268363484034635352)
XLA Ops:
  0.6 0.0 copy-start
  0.6 2.2 %copy-done = f32[16,16,4096]{2,1,0:T(8,128)S(1)} copy-done((f32[16,16,4096]{2,1,0:T(8,128)S(1)}, f32[16,16,4096]{2,1,0:T(8,128)}, u32[]{:S(2)}) %copy-start) | copy-done | bytes 4194328
  2.8 0.0 copy-start.1
  2.8 2.2 %copy-done.1 = f32[16,16,4096]{2,1,0:T(8,128)S(1)} copy-done((f32[16,16,4096]{2,1,0:T(8,128)S(1)}, f32[16,16,4096]{2,1,0:T(8,128)}, u32[]{:S(2)}) %copy-start.1) | copy-done | bytes 4194328
  5.0 0.0 copy-start.2
  5.0 0.9 copy-done.2
  6.0 106.6 %exchange.1 = (f32[16,128,512]{2,1,0:T(8,128)S(1)}, s32[128,512]{1,0:T(8,128)S(1)}, f32[128,128]{1,0:T(8,128)S(1)}, f32[24,512]{1,0:T(8,128)S(1)}, f32[24,512]{1,0:T(8,128)S(1)}, /*index=5*/f32[24,512]{1,0:T(8,128)S(1)}) custom-call(f32[16,16,4096]{2,1,0:T(8,128)S(1)} %copy-done, f32[16,16,4096]{2,1,0:T(8,128)S(1)} %copy-done.1, s32[16,4096]{1,0:T(8,128)S(1)} %copy-done.2), custom_call_target="tpu_custom_call" | custom-call | bytes 16777216 | tf_op jit(solution)/shard_map/exchange/pallas_call | solution.py:276
  112.6 6.9 %stencil.1 = (f32[16,128,512]{2,1,0:T(8,128)}, f32[16,128,512]{2,1,0:T(8,128)}) custom-call(f32[16,128,512]{2,1,0:T(8,128)S(1)} %get-tuple-element.8.tile_ref, s32[128,512]{1,0:T(8,128)S(1)} %get-tuple-element.9.bottom_ref, f32[128,128]{1,0:T(8,128)S(1)} %get-tuple-element.10.sides_ref, f32[24,512]{1,0:T(8,128)S(1)} %get-tuple-element.11.north_ref, ...), custom_call_target="tpu_custom_call" | custom-call | tf_op jit(solution)/shard_map/stencil/pallas_call | solution.py:309
Async XLA Ops:
  0.6 2.2 %copy-start = (f32[16,16,4096]{2,1,0:T(8,128)S(1)}, f32[16,16,4096]{2,1,0:T(8,128)}, u32[]{:S(2)}) copy-start(f32[16,16,4096]{2,1,0:T(8,128)} %warmth_ref.1) | copy-start | bytes 12582916
  2.8 2.2 %copy-start.1 = (f32[16,16,4096]{2,1,0:T(8,128)S(1)}, f32[16,16,4096]{2,1,0:T(8,128)}, u32[]{:S(2)}) copy-start(f32[16,16,4096]{2,1,0:T(8,128)} %salt_ref.1) | copy-start | bytes 12582916
  5.0 0.9 copy-start.2
where the time goes:
time: 121 us; the launch traced here: 119 us
  Pallas kernels  114 us (94%)
  local copies, waits for them, and re-layouts  5.32 us (4%)
    pallas_call x1, Pallas kernels, on_device(): pl.pallas_call(functools.partial(exchange, ny, nx, groups), out_shape=(ja...  107 us
    pallas_call x1, Pallas kernels, on_device(): pl.pallas_call(functools.partial(stencil, ny, levels, per), grid=(levels...  6.89 us
    unnamed x6, local copies, waits for them, and re-layouts  5.32 us

commit v1 on v0

--- a/solution.py
+++ b/solution.py
@@ -18,6 +18,8 @@
 MESH = pl.DeviceIdType.MESH
 LANES = 128
 MIB = 1 << 20
+roll = pltpu.roll
+GRANT = 32 * MIB
 
 
 def density(warmth, salt, wet, height):
@@ -29,12 +31,75 @@
     return jnp.where(wet, anomaly, 0.0)
 
 
+def swapped(cells, j):
+    lane = lax.broadcasted_iota(jnp.int32, (8, LANES), 1)
+    sub = lax.broadcasted_iota(jnp.int32, (8, LANES), 0)
+    if j >= 10:
+        return [cells[v ^ (1 << (j - 10))] for v in range(len(cells))]
+    axis, size, place, bit = (1, LANES, lane, 1 << j) if j < 7 else (0, 8, sub, 1 << (j - 7))
+    if 2 * bit == size:
+        return [roll(c, bit, axis) for c in cells]
+    upper = (place & bit) != 0
+    return [jnp.where(upper, roll(c, bit, axis), roll(c, size - bit, axis)) for c in cells]
+
+
+def stages_of(count):
+    return 10 + count.bit_length() - 1
+
+
+def routes(wet):
+    count = len(wet)
+    flags = jnp.concatenate([jnp.where(w, 1.0, 0.0) for w in wet], axis=0)
+    height = flags.shape[0]
+    upper = lax.broadcasted_iota(jnp.int32, (LANES, LANES), 0) <= lax.broadcasted_iota(jnp.int32, (LANES, LANES), 1)
+    lower = lax.broadcasted_iota(jnp.int32, (height, height), 1) < lax.broadcasted_iota(jnp.int32, (height, height), 0)
+    upto = jnp.dot(flags, jnp.where(upper, 1.0, 0.0), preferred_element_type=jnp.float32)
+    totals = jnp.broadcast_to(upto[:, LANES - 1:], (height, LANES))
+    before = jnp.dot(jnp.where(lower, 1.0, 0.0), totals, preferred_element_type=jnp.float32)
+    rank = jnp.where(flags > 0.0, (before + upto - flags).astype(jnp.int32), -1)
+    ranks = [rank[8 * v:8 * v + 8] for v in range(count)]
+    lane = lax.broadcasted_iota(jnp.int32, (8, LANES), 1)
+    sub = lax.broadcasted_iota(jnp.int32, (8, LANES), 0)
+    packing = [jnp.zeros((8, LANES), jnp.int32)] * count
+    unpacking = [jnp.zeros((8, LANES), jnp.int32)] * count
+    for j in range(stages_of(count)):
+        others = swapped(ranks, j)
+        following = []
+        for v in range(count):
+            here = (lane >> j) & 1 if j < 7 else (sub >> (j - 7)) & 1 if j < 10 else (v >> (j - 10)) & 1
+            mine, other = ranks[v], others[v]
+            takes = jnp.where(other >= 0, ((other >> j) & 1) ^ here, 1) == 0
+            stays = jnp.where(mine >= 0, ((mine >> j) & 1) ^ here, 1) == 0
+            leaves = jnp.where(mine >= 0, ((mine >> j) & 1) ^ here, 0) == 1
+            packing[v] = jnp.where(takes, packing[v] | (1 << j), packing[v])
+            unpacking[v] = jnp.where(leaves, unpacking[v] | (1 << j), unpacking[v])
+            following.append(jnp.where(takes, other, jnp.where(stays, mine, -1)))
+        ranks = following
+    return packing, unpacking
+
+
+def moved(layers, masks, order):
+    for j in order:
+        takes = [(mask & (1 << j)) != 0 for mask in masks]
+        layers = [
+            [jnp.where(t, o, c) for t, o, c in zip(takes, swapped(cells, j), cells)] for cells in layers
+        ]
+    return layers
+
+
+def pieces(block):
+    tall, wide = block.shape
+    return [
+        block[r:r + 8, c:c + LANES] for r in range(0, tall, 8) for c in range(0, wide, LANES)
+    ]
+
+
 def exchange(
     ny, nx, groups,
     warmth_ref, salt_ref, tally_ref,
     tile_ref, bottom_ref, sides_ref, north_ref, south_ref, fold_ref,
-    warmth, salt, tally, dens, pack, slab, slab_bottom, low, high,
-    load_sem, send_sem, recv_sem, bsend_sem, brecv_sem, psend_sem, precv_sem, own_sem, slab_sem, hsend_sem, hrecv_sem,
+    warmth, salt, tally, dens, pack, outbox, inbox, packing, unpacking, low, high,
+    load_sem, send_sem, recv_sem, bsend_sem, brecv_sem, psend_sem, precv_sem, own_sem, hsend_sem, hrecv_sem,
 ):
     y, x = lax.axis_index("ty"), lax.axis_index("tx")
     levels, band, width = dens.shape
@@ -81,7 +146,7 @@
         t = x ^ m
         part = pl.ds(g * depth, depth)
         return pltpu.make_async_remote_copy(
-            src_ref=dens.at[part, :, columns(t)], dst_ref=tile_ref.at[part, mine],
+            src_ref=outbox.at[t, part], dst_ref=inbox.at[x, part],
             send_sem=send_sem.at[g, m], recv_sem=recv_sem.at[g, x], device_id=(y, t), device_id_type=MESH)
 
     def pack_copy(m):
@@ -116,7 +181,31 @@
         pack[t] = cells
         return 0
 
-    lax.fori_loop(0, nx, fill, 0)
+    count = band * wide // (8 * LANES)
+    kept = outbox.shape[2] // 8
+    stages = stages_of(count)
+
+    def plan(m, _):
+        t = x ^ m
+        wet = [piece > 0 for piece in pieces(tally[:, columns(t)])]
+        for v, mask in enumerate(routes(wet)[0]):
+            packing[t, v] = mask
+        return 0
+
+    def gather(g, first):
+        def block(i, _):
+            t = x ^ (first - i)
+            masks = [packing[t, v] for v in range(count)]
+            for k0 in range(0, depth, 2):
+                ks = [g * depth + k for k in range(k0, min(k0 + 2, depth))]
+                layers = moved([pieces(dens[k, :, columns(t)]) for k in ks], masks, range(stages))
+                for k, cells in zip(ks, layers):
+                    for v in range(kept):
+                        outbox[t, k, 8 * v:8 * v + 8, :] = cells[v]
+            return 0
+        return block
+
+    lax.fori_loop(1, nx, plan, 0)
 
     def level(k, _):
         height = 5.0 + 10.0 * k.astype(jnp.float32)
@@ -125,10 +214,6 @@
             cols = columns(t)
             value = density(warmth[k, :, cols], salt[k, :, cols], k < tally[:, cols], height)
             dens[k, :, cols] = value
-            after = lax.rem(t + 1, nx)
-            before = lax.rem(t + nx - 1, nx)
-            pack[after] = jnp.where(lane == k, jnp.broadcast_to(value[:, wide - 1:], (band, LANES)), pack[after])
-            pack[before] = jnp.where(lane == levels + k, jnp.broadcast_to(value[:, :1], (band, LANES)), pack[before])
             return 0
 
         lax.fori_loop(0, nx, block, 0)
@@ -138,8 +223,26 @@
         for copy in loads[g]:
             copy.wait()
         lax.fori_loop(g * depth, (g + 1) * depth, level, 0)
+        lax.fori_loop(0, len(far), gather(g, far[0]), 0)
         for m in far:
             dens_copy(g, m).start()
+        lax.fori_loop(0, len(near), gather(g, near[0]), 0)
+    lax.fori_loop(0, nx, fill, 0)
+
+    def edges(t, _):
+        before = lax.rem(t + nx - 1, nx)
+        after = lax.rem(t + 1, nx)
+        before_cols = pl.ds(pl.multiple_of(before * wide + wide - LANES, LANES), LANES)
+        after_cols = pl.ds(pl.multiple_of(after * wide, LANES), LANES)
+        cells = pack[t]
+        for k in range(levels):
+            left = jnp.broadcast_to(dens[k, :, before_cols][:, LANES - 1:], (band, LANES))
+            right = jnp.broadcast_to(dens[k, :, after_cols][:, :1], (band, LANES))
+            cells = jnp.where(lane == k, left, jnp.where(lane == levels + k, right, cells))
+        pack[t] = cells
+        return 0
+
+    lax.fori_loop(0, nx, edges, 0)
     own[0].start()
     own[2].start()
     for g in range(groups):
@@ -150,33 +253,50 @@
 
     own[0].wait()
     own[1].wait()
-
-    def arrive(s):
+    for m in far + near:
+        bottom_copy(m).wait_send()
+    for s in range(nx):
         @pl.when(x != s)
         def _():
             pltpu.make_async_copy(bottom_ref.at[rows(s)], bottom_ref.at[rows(s)], brecv_sem.at[s]).wait()
-            for g in range(groups):
-                part = tile_ref.at[pl.ds(g * depth, depth), rows(s)]
-                pltpu.make_async_copy(part, part, recv_sem.at[g, s]).wait()
-
-    arrive(0)
-    arrive(nx - 1)
-    top = nx * band - 8
-    slabs = [
-        pltpu.make_async_copy(tile_ref.at[:, pl.ds(0, 8)], slab.at[0], slab_sem.at[0]),
-        pltpu.make_async_copy(tile_ref.at[:, pl.ds(top, 8)], slab.at[1], slab_sem.at[1]),
-        pltpu.make_async_copy(bottom_ref.at[pl.ds(0, 8)], slab_bottom.at[0], slab_sem.at[2]),
-        pltpu.make_async_copy(bottom_ref.at[pl.ds(top, 8)], slab_bottom.at[1], slab_sem.at[3]),
-    ]
-    for copy in slabs:
-        copy.start()
-    for copy in slabs:
-        copy.wait()
+
+    def unplan(m, _):
+        s = x ^ m
+        wet = [piece > 0 for piece in pieces(bottom_ref[rows(s), :])]
+        for v, mask in enumerate(routes(wet)[1]):
+            unpacking[s, v] = mask
+        return 0
+
+    lax.fori_loop(1, nx, unplan, 0)
+
+    def spread(first, number):
+        def block(q, _):
+            g, s = q // number, x ^ (first - q % number)
+            part = inbox.at[s, pl.ds(g * depth, depth)]
+            pltpu.make_async_copy(part, part, recv_sem.at[g, s]).wait()
+            masks = [unpacking[s, v] for v in range(count)]
+            blank = [jnp.zeros((8, LANES), jnp.float32)] * (count - kept)
+            for k0 in range(0, depth, 2):
+                ks = [g * depth + k for k in range(k0, min(k0 + 2, depth))]
+                layers = [[inbox[s, k, 8 * v:8 * v + 8, :] for v in range(kept)] + blank for k in ks]
+                layers = moved(layers, masks, range(stages - 1, -1, -1))
+                for k, cells in zip(ks, layers):
+                    for r in range(0, band, 8):
+                        line = r // 8 * (wide // LANES)
+                        value = jnp.concatenate(cells[line:line + wide // LANES], axis=1)
+                        at = pl.ds(pl.multiple_of(s * band + r, 8), 8)
+                        tile_ref[k, at, :] = jnp.where(k < bottom_ref[at, :], value, 0.0)
+            return 0
+        return block
+
+    lax.fori_loop(0, groups * len(far), spread(far[0], len(far)), 0)
+    lax.fori_loop(0, groups * len(near), spread(near[0], len(near)), 0)
+    tall = nx * band
     for k in range(levels):
-        low[k:k + 1, :] = slab[0, k, 0:1, :]
-        high[k:k + 1, :] = slab[1, k, 7:8, :]
-    low[levels:, :] = jnp.broadcast_to(slab_bottom[0, 0:1, :].astype(jnp.float32), (8, wide))
-    high[levels:, :] = jnp.broadcast_to(slab_bottom[1, 7:8, :].astype(jnp.float32), (8, wide))
+        low[k:k + 1, :] = tile_ref[k, 0:1, :]
+        high[k:k + 1, :] = tile_ref[k, tall - 1:tall, :]
+    low[levels:, :] = jnp.broadcast_to(bottom_ref[0:1, :].astype(jnp.float32), (8, wide))
+    high[levels:, :] = jnp.broadcast_to(bottom_ref[tall - 1:tall, :].astype(jnp.float32), (8, wide))
 
     def halo(index, src, dst, target):
         return pltpu.make_async_remote_copy(
@@ -193,8 +313,6 @@
     def _():
         across.start()
 
-    for s in range(1, nx - 1):
-        arrive(s)
     for s in range(nx):
         @pl.when(x != s)
         def _():
@@ -208,7 +326,6 @@
         across.wait()
 
     for m in far + near:
-        bottom_copy(m).wait_send()
         pack_copy(m).wait_send()
         for g in range(groups):
             dens_copy(g, m).wait_send()
@@ -269,7 +386,10 @@
     levels, band, width = potential_warmth.shape
     wide, tall = width // nx, band * nx
     groups = 4 if levels % 4 == 0 else 1
-    hbm = pl.BlockSpec(memory_space=pl.ANY)
+    count = band * wide // (8 * LANES)
+    kept = 8 * (3 * count // 4)
+    hbm = pl.BlockSpec(memory_space=pltpu.HBM)
+    vmem = pl.BlockSpec(memory_space=pltpu.VMEM)
     f32, i32 = jnp.float32, jnp.int32
     edge = jax.ShapeDtypeStruct((levels + 8, wide), f32)
     dma = pltpu.SemaphoreType.DMA
@@ -282,23 +402,25 @@
             edge, edge, edge,
         ),
         in_specs=[hbm] * 3,
-        out_specs=(hbm,) * 6,
+        out_specs=(vmem,) * 6,
         scratch_shapes=[
             pltpu.VMEM((levels, band, width), f32),
             pltpu.VMEM((levels, band, width), f32),
             pltpu.VMEM((band, width), i32),
             pltpu.VMEM((levels, band, width), f32),
             pltpu.VMEM((nx, band, LANES), f32),
-            pltpu.VMEM((2, levels, 8, wide), f32),
-            pltpu.VMEM((2, 8, wide), i32),
+            pltpu.VMEM((nx, levels, kept, LANES), f32),
+            pltpu.VMEM((nx, levels, kept, LANES), f32),
+            pltpu.VMEM((nx, count, 8, LANES), i32),
+            pltpu.VMEM((nx, count, 8, LANES), i32),
             pltpu.VMEM((levels + 8, wide), f32),
             pltpu.VMEM((levels + 8, wide), f32),
             dma((2 * groups + 1,)),
             dma((groups, nx)), dma((groups, nx)),
             dma((nx,)), dma((nx,)), dma((nx,)), dma((nx,)),
-            dma((3,)), dma((4,)), dma((3,)), dma((3,)),
+            dma((3,)), dma((3,)), dma((3,)),
         ],
-        compiler_params=pltpu.CompilerParams(collective_id=0, has_side_effects=True, vmem_limit_bytes=24 * MIB),
+        compiler_params=pltpu.CompilerParams(collective_id=0, has_side_effects=True, vmem_limit_bytes=GRANT),
         cost_estimate=pl.CostEstimate(flops=0, bytes_accessed=16 * levels * band * width, transcendentals=0),
         name="exchange",
     )(potential_warmth, saltiness_field, ocean_tier_tally)

time: 121 us -> 112 us (0.926)
  Pallas kernels: 114 us -> 105 us
    pallas_call x1, Pallas kernels: 107 us -> 98.5 us  [on_device(): pl.pallas_call(functools.partial(exchange, ny, nx, groups), out_shape=(ja...]
where the time goes in v1:
time: 112 us; the launch traced here: 111 us
  Pallas kernels  105 us (94%)
  local copies, waits for them, and re-layouts  5.32 us (5%)
    pallas_call x1, Pallas kernels, on_device(): pl.pallas_call(functools.partial(exchange, ny, nx, groups), out_shape=(ja...  98.5 us
    pallas_call x1, Pallas kernels, on_device(): pl.pallas_call(functools.partial(stencil, ny, levels, per), grid=(levels...  6.89 us
    unnamed x6, local copies, waits for them, and re-layouts  5.32 us

profile of v1, /device:TPU:1, one launch (start us, length us, event | category | flops | bytes accessed | tf_op | source)
XLA Modules:
  0.0 111.3 jit_solution(6845138719467396695)
XLA Ops:
  0.6 0.0 copy-start
  0.6 2.2 %copy-done = f32[16,16,4096]{2,1,0:T(8,128)S(1)} copy-done((f32[16,16,4096]{2,1,0:T(8,128)S(1)}, f32[16,16,4096]{2,1,0:T(8,128)}, u32[]{:S(2)}) %copy-start) | copy-done | bytes 4194328
  2.8 0.0 copy-start.1
  2.8 2.2 %copy-done.1 = f32[16,16,4096]{2,1,0:T(8,128)S(1)} copy-done((f32[16,16,4096]{2,1,0:T(8,128)S(1)}, f32[16,16,4096]{2,1,0:T(8,128)}, u32[]{:S(2)}) %copy-start.1) | copy-done | bytes 4194328
  5.0 0.0 copy-start.2
  5.0 0.9 copy-done.2
  6.0 98.5 %exchange.1 = (f32[16,128,512]{2,1,0:T(8,128)S(1)}, s32[128,512]{1,0:T(8,128)S(1)}, f32[128,128]{1,0:T(8,128)S(1)}, f32[24,512]{1,0:T(8,128)S(1)}, f32[24,512]{1,0:T(8,128)S(1)}, /*index=5*/f32[24,512]{1,0:T(8,128)S(1)}) custom-call(f32[16,16,4096]{2,1,0:T(8,128)S(1)} %copy-done, f32[16,16,4096]{2,1,0:T(8,128)S(1)} %copy-done.1, s32[16,4096]{1,0:T(8,128)S(1)} %copy-done.2), custom_call_target="tpu_custom_call" | custom-call | bytes 16777216 | tf_op jit(solution)/shard_map/exchange/pallas_call | solution.py:396
  104.4 6.9 %stencil.1 = (f32[16,128,512]{2,1,0:T(8,128)}, f32[16,128,512]{2,1,0:T(8,128)}) custom-call(f32[16,128,512]{2,1,0:T(8,128)S(1)} %get-tuple-element.8.tile_ref, s32[128,512]{1,0:T(8,128)S(1)} %get-tuple-element.9.bottom_ref, f32[128,128]{1,0:T(8,128)S(1)} %get-tuple-element.10.sides_ref, f32[24,512]{1,0:T(8,128)S(1)} %get-tuple-element.11.north_ref, ...), custom_call_target="tpu_custom_call" | custom-call | tf_op jit(solution)/shard_map/stencil/pallas_call | solution.py:431
Async XLA Ops:
  0.6 2.2 %copy-start = (f32[16,16,4096]{2,1,0:T(8,128)S(1)}, f32[16,16,4096]{2,1,0:T(8,128)}, u32[]{:S(2)}) copy-start(f32[16,16,4096]{2,1,0:T(8,128)} %warmth_ref.1) | copy-start | bytes 12582916
  2.8 2.2 %copy-start.1 = (f32[16,16,4096]{2,1,0:T(8,128)S(1)}, f32[16,16,4096]{2,1,0:T(8,128)}, u32[]{:S(2)}) copy-start(f32[16,16,4096]{2,1,0:T(8,128)} %salt_ref.1) | copy-start | bytes 12582916
  5.0 0.9 copy-start.2

commit v2 on v1

--- a/solution.py
+++ b/solution.py
@@ -19,7 +19,7 @@
 LANES = 128
 MIB = 1 << 20
 roll = pltpu.roll
-GRANT = 32 * MIB
+GRANT = 46 * MIB
 
 
 def density(warmth, salt, wet, height):
@@ -163,11 +163,26 @@
     far = [m for m in range(nx - 1, 0, -1) if m >= nx // 2]
     near = [m for m in range(nx - 1, 0, -1) if m < nx // 2]
 
+    def level(k, _):
+        height = 5.0 + 10.0 * k.astype(jnp.float32)
+
+        def block(t, _):
+            cols = columns(t)
+            value = density(warmth[k, :, cols], salt[k, :, cols], k < tally[:, cols], height)
+            dens[k, :, cols] = value
+            return 0
+
+        lax.fori_loop(0, nx, block, 0)
+        return 0
+
+    load_tally.wait()
+    for copy in loads[0]:
+        copy.wait()
+    lax.fori_loop(0, depth, level, 0)
     pl.semaphore_wait(barrier, nx - 1 + 2)
     for m in far + near:
         bottom_copy(m).start()
     own[1].start()
-    load_tally.wait()
 
     lane = lax.broadcasted_iota(jnp.int32, (band, LANES), 1)
 
@@ -205,27 +220,18 @@
             return 0
         return block
 
-    lax.fori_loop(1, nx, plan, 0)
-
-    def level(k, _):
-        height = 5.0 + 10.0 * k.astype(jnp.float32)
-
-        def block(t, _):
-            cols = columns(t)
-            value = density(warmth[k, :, cols], salt[k, :, cols], k < tally[:, cols], height)
-            dens[k, :, cols] = value
-            return 0
-
-        lax.fori_loop(0, nx, block, 0)
-        return 0
+    lax.fori_loop(nx // 2, nx, plan, 0)
 
     for g in range(groups):
-        for copy in loads[g]:
-            copy.wait()
-        lax.fori_loop(g * depth, (g + 1) * depth, level, 0)
+        if g > 0:
+            for copy in loads[g]:
+                copy.wait()
+            lax.fori_loop(g * depth, (g + 1) * depth, level, 0)
         lax.fori_loop(0, len(far), gather(g, far[0]), 0)
         for m in far:
             dens_copy(g, m).start()
+        if g == 0:
+            lax.fori_loop(1, nx // 2, plan, 0)
         lax.fori_loop(0, len(near), gather(g, near[0]), 0)
     lax.fori_loop(0, nx, fill, 0)
 

time: 112 us -> 103 us (0.920)
  local copies, waits for them, and re-layouts: 5.32 us -> 0.94 us
  Pallas kernels: 105 us -> 101 us
    unnamed x6 -> x2, local copies, waits for them, and re-layouts: 5.32 us -> 0.94 us
    pallas_call x1, Pallas kernels: 98.5 us -> 94.2 us  [on_device(): pl.pallas_call(functools.partial(exchange, ny, nx, groups), out_shape=(ja...]
where the time goes in v2:
time: 103 us
  Pallas kernels  101 us (98%)
    pallas_call x1, Pallas kernels, on_device(): pl.pallas_call(functools.partial(exchange, ny, nx, groups), out_shape=(ja...  94.2 us
    pallas_call x1, Pallas kernels, on_device(): pl.pallas_call(functools.partial(stencil, ny, levels, per), grid=(levels...  6.89 us

profile of v2, /device:TPU:1, one launch (start us, length us, event | category | flops | bytes accessed | tf_op | source)
XLA Modules:
  0.0 102.7 jit_solution(13248766974955790786)
XLA Ops:
  0.6 0.0 copy-start
  0.6 0.9 copy-done
  1.6 94.2 %exchange.1 = (f32[16,128,512]{2,1,0:T(8,128)S(1)}, s32[128,512]{1,0:T(8,128)S(1)}, f32[128,128]{1,0:T(8,128)S(1)}, f32[24,512]{1,0:T(8,128)S(1)}, f32[24,512]{1,0:T(8,128)S(1)}, /*index=5*/f32[24,512]{1,0:T(8,128)S(1)}) custom-call(f32[16,16,4096]{2,1,0:T(8,128)} %warmth_ref.1, f32[16,16,4096]{2,1,0:T(8,128)} %salt_ref.1, s32[16,4096]{1,0:T(8,128)S(1)} %copy-done), custom_call_target="tpu_custom_call" | custom-call | bytes 16777216 | tf_op jit(solution)/shard_map/exchange/pallas_call | solution.py:402
  95.8 6.9 %stencil.1 = (f32[16,128,512]{2,1,0:T(8,128)}, f32[16,128,512]{2,1,0:T(8,128)}) custom-call(f32[16,128,512]{2,1,0:T(8,128)S(1)} %get-tuple-element.8.tile_ref, s32[128,512]{1,0:T(8,128)S(1)} %get-tuple-element.9.bottom_ref, f32[128,128]{1,0:T(8,128)S(1)} %get-tuple-element.10.sides_ref, f32[24,512]{1,0:T(8,128)S(1)} %get-tuple-element.11.north_ref, ...), custom_call_target="tpu_custom_call" | custom-call | tf_op jit(solution)/shard_map/stencil/pallas_call | solution.py:437
Async XLA Ops:
  0.6 1.0 copy-start
